TPU v7x, 32 devices: a whole 2x2x4 slice. The times are simulated.
32 devices in a mesh: row: 2 (over core), sector: 4 (over z), slab: 4 (over y, x).
Axes of the slice: x: 2, y: 2, z: 4, core: 2. Of those that a mesh axis runs over, the one named last changes fastest.
Arguments:
- state: float32 [2, 5, 32, 128, 128], P('row', None, 'slab', 'sector'), may hold values from -6 to 6
- source: float32 [2, 5, 32, 128, 128], P('row', None, 'slab', 'sector'), may hold values from -6 to 6
- diag_inverse: float32 [2, 5, 5, 32, 128, 128], P('row', None, None, 'slab', 'sector'), may hold values from -1 to 1
- jac_axial: float32 [2, 5, 5], P('row'), may hold values from -1 to 2
- jac_cross: float32 [2, 2, 5, 5], P('row'), may hold values from -2.5 to 2.5
- owner: int32 [128], replicated, may hold values from 0 to 127, as said below
Outputs:
- residual: float32 [2, 5, 32, 128, 128], P('row', None, 'slab', 'sector')
- new_state: float32 [2, 5, 32, 128, 128], P('row', None, 'slab', 'sector')
Inputs may be any that keep to these rules, and one draw needn't show every extreme that they name: owner is a permutation; for some whole s, the columns b * 32 to b * 32 + 31 of the rotor face exactly the stator columns s + b * 32 to s + b * 32 + 31, taken modulo 128, for every b.
All inputs are finite; a program needn't handle non-finite values.
Results may differ from a plain program's by a relative error of at most 0.0001.
Values sent between devices are 32-bit elements; how exact they have to be, the bound alone decides.
A program may use at most 64 MiB of HBM per device.

v0:
```python
import jax
import jax.numpy as jnp
from jax import lax
from jax.sharding import PartitionSpec as P

exact_mode = lax.Precision.HIGHEST


def extended(block, sides, width, periodic):
    for axis, dim in sides:
        count = lax.axis_size(axis)
        forward = [(i, i + 1) for i in range(count - 1)]
        if periodic:
            forward.append((count - 1, 0))
        backward = [(target, source) for source, target in forward]
        low = lax.ppermute(
            lax.slice_in_dim(block, block.shape[dim] - width, None, axis=dim), axis, forward
        )
        high = lax.ppermute(lax.slice_in_dim(block, 0, width, axis=dim), axis, backward)
        block = jnp.concatenate([low, block, high], axis=dim)
    return block


def shifted(block, axis, distance):
    devices = range(lax.axis_size(axis))
    route = [(i - distance, i) for i in devices if i - distance in devices]
    return lax.ppermute(block, axis, route)


def mix_const(matrix, field):
    return jnp.einsum("ij,j...->i...", matrix, field, precision=exact_mode)


def per_cell(blocks, field):
    return jnp.sum(blocks * field[None], axis=1)


def forward_sweep(residual, inverse, axial, entering):
    previous = entering
    plane_list = []
    for plane_at in range(residual.shape[1]):
        present_plane = per_cell(
            inverse[:, :, plane_at], residual[:, plane_at] + 0.5 * mix_const(axial, previous)
        )
        plane_list.append(present_plane)
        previous = present_plane
    return jnp.stack(plane_list, axis=1)


def backward_sweep(provisional, inverse, axial, entering):
    planes = provisional.shape[1]
    following = entering
    plane_list = []
    for step_at in range(planes):
        plane_at = planes - 1 - step_at
        present_plane = provisional[:, plane_at] - per_cell(
            inverse[:, :, plane_at], 0.5 * mix_const(axial, following)
        )
        plane_list.append(present_plane)
        following = present_plane
    return jnp.stack(plane_list[::-1], axis=1)


def per_device(state, source, diag_inverse, jac_axial, jac_cross, owner):
    field = state[0]
    inverse = diag_inverse[0]
    axial = jac_axial[0]
    circular = jac_cross[0, 0]
    radial_jac = jac_cross[0, 1]
    planes = field.shape[1]
    columns = field.shape[2]
    radial_cells = field.shape[3]
    total_columns = owner.shape[0]
    blade_row_index = lax.axis_index("row")
    slab_index = lax.axis_index("slab")
    sector_index = lax.axis_index("sector")
    slabs = lax.axis_size("slab")
    axial_padded = extended(field, ((("row", "slab"), 1),), 1, False)
    below = axial_padded[:, 0]
    above = axial_padded[:, planes + 1]
    partner = jnp.where(blade_row_index == 0, above, below)
    doubled = jnp.concatenate([owner, owner])
    local_ids = sector_index * columns + jnp.arange(columns, dtype=jnp.int32)
    owner_local = lax.dynamic_slice_in_dim(doubled, sector_index * columns, columns)
    candidates = lax.all_gather(partner, "sector", axis=1, tiled=True)
    candidate_ids = jnp.arange(total_columns, dtype=jnp.int32)
    rotor_hits = owner_local[:, None] == candidate_ids[None, :]
    stator_hits = owner[None, :] == local_ids[:, None]
    section_chooser = jnp.where(blade_row_index == 0, rotor_hits, stator_hits).astype(jnp.float32)
    ghost = jnp.einsum("jk,vkr->vjr", section_chooser, candidates, precision=exact_mode)
    rotor_top = (blade_row_index == 0) & (slab_index == slabs - 1)
    stator_foot = (blade_row_index == 1) & (slab_index == 0)
    upper = jnp.where(rotor_top, ghost, above)
    lower = jnp.where(stator_foot, ghost, below)
    axial_diff = jnp.concatenate([field[:, 1:], upper[:, None]], axis=1) - jnp.concatenate(
        [lower[:, None], field[:, :-1]], axis=1
    )
    cycle = extended(field, (("sector", 2),), 1, True)
    cycle_diff = cycle[:, :, 2:] - cycle[:, :, :-2]
    radial = jnp.pad(field, ((0, 0), (0, 0), (0, 0), (1, 1)))
    radial_diff = radial[..., 2:] - radial[..., :-2]
    residual = source[0] - 0.5 * (
        mix_const(axial, axial_diff)
        + mix_const(circular, cycle_diff)
        + mix_const(radial_jac, radial_diff)
    )
    zeros_plane = jnp.zeros((5, columns, radial_cells), jnp.float32)
    entering = zeros_plane
    for section_lookup in range(slabs - 1):
        provisional = forward_sweep(residual, inverse, axial, entering)
        entering = shifted(provisional[:, -1], "slab", 1)
    provisional = forward_sweep(residual, inverse, axial, entering)
    entering = zeros_plane
    for section_lookup in range(slabs - 1):
        update = backward_sweep(provisional, inverse, axial, entering)
        entering = shifted(update[:, 0], "slab", -1)
    update = backward_sweep(provisional, inverse, axial, entering)
    return (residual[None], (field + update)[None])


def solution(mesh):
    return jax.shard_map(
        per_device,
        mesh=mesh,
        in_specs=(
            P("row", None, "slab", "sector", None),
            P("row", None, "slab", "sector", None),
            P("row", None, None, "slab", "sector", None),
            P("row", None, None),
            P("row", None, None, None),
            P(),
        ),
        out_specs=(P("row", None, "slab", "sector", None), P("row", None, "slab", "sector", None)),
        check_vma=False,
    )
```

profile of v0, /device:TPU:0, one launch (start us, length us, event | category | flops | bytes accessed | tf_op | source)
XLA Modules:
  0.0 107.5 jit_solution(4227483769644810466)
XLA Ops:
  0.6 1.1 %copy.632 = f32[1,5,8,32,128]{4,3,1,2,0:T(8,128)S(1)} copy(f32[1,5,8,32,128]{4,3,2,1,0:T(8,128)} %param.6) | data formatting | bytes 1310720 | tf_op args[0]
  1.8 1.3 %collective-permute-start = (f32[5,1,32,128]{3,2,0,1:T(8,128)S(1)}, f32[5,1,32,128]{3,2,0,1:T(8,128)S(1)}, u32[]{:S(2)}, u32[]{:S(2)}) collective-permute-start(f32[5,1,32,128]{3,2,0,1:T(8,128)S(1)} %get-tuple-element.18), channel_id=1, source_target_pairs={{1,0},{2,1},{3,2},{16,3},{17,16},{18,17},{19,18},{5,4},{6,5},{7,6}... | collective-permute-start | bytes 245768 | tf_op jit(solution)/shard_map/ppermute | solution.py:19
  3.1 5.5 %collective-permute-start.1 = (f32[5,1,32,128]{3,2,0,1:T(8,128)S(1)}, f32[5,1,32,128]{3,2,0,1:T(8,128)S(1)}, u32[]{:S(2)}, u32[]{:S(2)}) collective-permute-start(f32[5,1,32,128]{3,2,0,1:T(8,128)S(1)} %get-tuple-element.19), channel_id=1, source_target_pairs={{0,1},{1,2},{2,3},{3,16},{16,17},{17,18},{18,19},{4,5},{5,6},{6,7}... | collective-permute-start | bytes 245768 | tf_op jit(solution)/shard_map/ppermute | solution.py:16
  8.7 4.2 %collective-permute-start.2 = (f32[5,8,1,128]{3,2,0,1:T(1,128)S(1)}, f32[5,8,1,128]{3,2,0,1:T(1,128)S(1)}, u32[]{:S(2)}, u32[]{:S(2)}) collective-permute-start(f32[5,8,1,128]{3,2,0,1:T(1,128)S(1)} %get-tuple-element.14), channel_id=1, source_target_pairs={{4,0},{8,4},{12,8},{0,12},{5,1},{9,5},{13,9},{1,13},{6,2},{10,6},{... | collective-permute-start | bytes 61448 | tf_op jit(solution)/shard_map/ppermute | solution.py:19
  13.2 1.2 %collective-permute-done.2 = f32[5,8,1,128]{3,2,0,1:T(1,128)S(1)} collective-permute-done((f32[5,8,1,128]{3,2,0,1:T(1,128)S(1)}, f32[5,8,1,128]{3,2,0,1:T(1,128)S(1)}, u32[]{:S(2)}, u32[]{:S(2)}) %collective-permute-start.2) | collective-permute-done | bytes 20512 | tf_op jit(solution)/shard_map/ppermute | solution.py:19
  14.3 4.1 %collective-permute-done.3 = f32[5,8,1,128]{3,2,0,1:T(1,128)S(1)} collective-permute-done((f32[5,8,1,128]{3,2,0,1:T(1,128)S(1)}, f32[5,8,1,128]{3,2,0,1:T(1,128)S(1)}, u32[]{:S(2)}, u32[]{:S(2)}) %collective-permute-start.3) | collective-permute-done | bytes 20512 | tf_op jit(solution)/shard_map/ppermute | solution.py:16
  18.4 0.5 fusion.101
  19.0 14.3 %all_gather.3 = f32[5,128,128]{2,1,0:T(8,128)S(1)} all-gather(f32[5,32,128]{2,1,0:T(8,128)S(1)} %bitcast_select_fusion.1), channel_id=1, replica_groups=mesh['row'=2,'sector'=4,'slab'=4] {'sector'}, dimensions={1}, use_global_device_ids=true | all-gather | bytes 409600 | tf_op jit(solution)/shard_map/all_gather | solution.py:85
  33.7 1.4 %fusion.99 = f32[8,32,128,5]{2,3,1,0:T(8,128)S(1)} fusion(f32[5,8,32,128]{3,2,0,1:T(8,128)S(1)} %maximum_subtract_fusion, f32[1,5,5]{2,0,1:T(1,128)S(1)} %copy-done.1), kind=kOutput, calls=%fused_computation.167 | convolution fusion | flops 9830400 | bytes 1310820 | tf_op jit(solution)/shard_map/ij,j...->i.../dot_general | solution.py:31
  35.1 1.4 %convolution_add_fusion.1 = f32[8,32,128,5]{2,3,1,0:T(8,128)S(1)} fusion(f32[8,32,128,5]{2,3,1,0:T(8,128)S(1)} %fusion.99, f32[5,8,32,128]{3,2,0,1:T(8,128)S(1)} %get-tuple-element.13, f32[1,1,5,5]{3,1,2,0:T(1,128)S(1)} %get-tuple-element.23), kind=kOutput, calls=%fused_computation.6 | convolution fusion | flops 9994240 | bytes 1966180 | tf_op jit(solution)/shard_map/ij,j...->i.../dot_general | solution.py:31
  36.4 1.8 %fusion.2 = f32[5,8,32,128]{3,0,2,1:T(8,128)S(1)} fusion(f32[8,32,128,5]{2,3,1,0:T(8,128)S(1)} %convolution_add_fusion.1, f32[5,8,32,128]{3,2,0,1:T(8,128)S(1)} %get-tuple-element.12, f32[1,5,8,32,128]{4,3,2,1,0:T(8,128)S(1)} %copy-done.3, f32[1,1,5,5]{3,1,2,0:T(1,128)S(1)} %get-tuple-element.22), kind=kOutput, calls=%fused_computation.5 | convolution fusion | flops 10321920 | bytes 2621540 | tf_op jit(solution)/shard_map/ij,j...->i.../dot_general | solution.py:31
  38.6 0.3 fusion.66
  39.3 0.3 fusion.68
  39.7 0.3 fusion.69
  40.0 0.3 fusion.70
  40.4 0.3 fusion.71
  40.8 0.3 fusion.72
  41.2 4.1 %collective-permute-start.4 = (f32[5,32,128]{2,0,1:T(8,128)S(1)}, f32[5,32,128]{2,0,1:T(8,128)S(1)}, u32[]{:S(2)}, u32[]{:S(2)}) collective-permute-start(f32[5,32,128]{2,0,1:T(8,128)S(1)} %copy.310), channel_id=1, source_target_pairs={{0,1},{1,2},{2,3},{4,5},{5,6},{6,7},{8,9},{9,10},{10,11},{12,13},{... | collective-permute-start | bytes 245768 | tf_op jit(solution)/shard_map/ppermute | solution.py:27
  45.3 2.5 %collective-permute-done.4 = f32[5,32,128]{2,0,1:T(8,128)S(1)} collective-permute-done((f32[5,32,128]{2,0,1:T(8,128)S(1)}, f32[5,32,128]{2,0,1:T(8,128)S(1)}, u32[]{:S(2)}, u32[]{:S(2)}) %collective-permute-start.4) | collective-permute-done | bytes 81952 | tf_op jit(solution)/shard_map/ppermute | solution.py:27
  48.1 0.3 fusion.74
  48.5 0.3 fusion.75
  48.9 0.3 fusion.76
  49.6 0.3 fusion.78
  50.0 0.3 fusion.79
  50.4 0.3 fusion.80
  50.8 4.5 %collective-permute-start.5 = (f32[5,32,128]{2,0,1:T(8,128)S(1)}, f32[5,32,128]{2,0,1:T(8,128)S(1)}, u32[]{:S(2)}, u32[]{:S(2)}) collective-permute-start(f32[5,32,128]{2,0,1:T(8,128)S(1)} %copy.326), channel_id=1, source_target_pairs={{0,1},{1,2},{2,3},{4,5},{5,6},{6,7},{8,9},{9,10},{10,11},{12,13},{... | collective-permute-start | bytes 245768 | tf_op jit(solution)/shard_map/ppermute | solution.py:27
  55.4 2.3 %collective-permute-done.5 = f32[5,32,128]{2,0,1:T(8,128)S(1)} collective-permute-done((f32[5,32,128]{2,0,1:T(8,128)S(1)}, f32[5,32,128]{2,0,1:T(8,128)S(1)}, u32[]{:S(2)}, u32[]{:S(2)}) %collective-permute-start.5) | collective-permute-done | bytes 81952 | tf_op jit(solution)/shard_map/ppermute | solution.py:27
  58.0 0.3 fusion.82
  58.4 0.3 fusion.83
  58.7 0.3 fusion.84
  59.1 0.3 fusion.85
  59.5 0.3 fusion.86
  59.8 0.3 fusion.87
  60.2 0.3 fusion.88
  60.6 4.4 %collective-permute-start.6 = (f32[5,32,128]{2,0,1:T(8,128)S(1)}, f32[5,32,128]{2,0,1:T(8,128)S(1)}, u32[]{:S(2)}, u32[]{:S(2)}) collective-permute-start(f32[5,32,128]{2,0,1:T(8,128)S(1)} %copy.342), channel_id=1, source_target_pairs={{0,1},{1,2},{2,3},{4,5},{5,6},{6,7},{8,9},{9,10},{10,11},{12,13},{... | collective-permute-start | bytes 245768 | tf_op jit(solution)/shard_map/ppermute | solution.py:27
  65.0 2.5 %collective-permute-done.6 = f32[5,32,128]{2,0,1:T(8,128)S(1)} collective-permute-done((f32[5,32,128]{2,0,1:T(8,128)S(1)}, f32[5,32,128]{2,0,1:T(8,128)S(1)}, u32[]{:S(2)}, u32[]{:S(2)}) %collective-permute-start.6) | collective-permute-done | bytes 81952 | tf_op jit(solution)/shard_map/ppermute | solution.py:27
  68.2 0.3 fusion.91
  68.6 0.3 fusion.92
  68.9 0.3 fusion.93
  69.3 0.3 fusion.94
  69.7 0.3 fusion.95
  70.0 0.3 fusion.96
  70.4 0.3 fusion.33
  70.8 0.3 fusion.32
  71.2 0.3 fusion.31
  71.6 0.3 fusion.30
  72.0 0.3 fusion.29
  72.4 0.3 fusion.28
  72.8 0.3 fusion.27
  73.2 1.3 %collective-permute-start.7 = (f32[5,32,128]{2,0,1:T(8,128)S(1)}, f32[5,32,128]{2,0,1:T(8,128)S(1)}, u32[]{:S(2)}, u32[]{:S(2)}) collective-permute-start(f32[5,32,128]{2,0,1:T(8,128)S(1)} %copy_subtract_fusion), channel_id=1, source_target_pairs={{1,0},{2,1},{3,2},{5,4},{6,5},{7,6},{9,8},{10,9},{11,10},{13,12},{... | collective-permute-start | bytes 245768 | tf_op jit(solution)/shard_map/ppermute | solution.py:27
  74.5 6.0 %collective-permute-done.7 = f32[5,32,128]{2,0,1:T(8,128)S(1)} collective-permute-done((f32[5,32,128]{2,0,1:T(8,128)S(1)}, f32[5,32,128]{2,0,1:T(8,128)S(1)}, u32[]{:S(2)}, u32[]{:S(2)}) %collective-permute-start.7) | collective-permute-done | bytes 81952 | tf_op jit(solution)/shard_map/ppermute | solution.py:27
  80.9 0.3 fusion.25
  81.3 0.3 fusion.24
  81.7 0.3 fusion.23
  82.4 0.3 fusion.21
  82.8 0.3 fusion.20
  83.2 0.3 fusion.19
  83.7 1.3 %collective-permute-start.8 = (f32[5,32,128]{2,0,1:T(8,128)S(1)}, f32[5,32,128]{2,0,1:T(8,128)S(1)}, u32[]{:S(2)}, u32[]{:S(2)}) collective-permute-start(f32[5,32,128]{2,0,1:T(8,128)S(1)} %copy_subtract_fusion.1), channel_id=1, source_target_pairs={{1,0},{2,1},{3,2},{5,4},{6,5},{7,6},{9,8},{10,9},{11,10},{13,12},{... | collective-permute-start | bytes 245768 | tf_op jit(solution)/shard_map/ppermute | solution.py:27
  85.0 8.2 %collective-permute-done.8 = f32[5,32,128]{2,0,1:T(8,128)S(1)} collective-permute-done((f32[5,32,128]{2,0,1:T(8,128)S(1)}, f32[5,32,128]{2,0,1:T(8,128)S(1)}, u32[]{:S(2)}, u32[]{:S(2)}) %collective-permute-start.8) | collective-permute-done | bytes 81952 | tf_op jit(solution)/shard_map/ppermute | solution.py:27
  96.2 1.5 %collective-permute-start.9 = (f32[5,32,128]{2,1,0:T(8,128)S(1)}, f32[5,32,128]{2,1,0:T(8,128)S(1)}, u32[]{:S(2)}, u32[]{:S(2)}) collective-permute-start(f32[5,32,128]{2,1,0:T(8,128)S(1)} %sub.223), channel_id=1, source_target_pairs={{1,0},{2,1},{3,2},{5,4},{6,5},{7,6},{9,8},{10,9},{11,10},{13,12},{... | collective-permute-start | bytes 245768 | tf_op jit(solution)/shard_map/ppermute | solution.py:27
  97.8 1.0 copy.424
  98.7 4.5 %collective-permute-done.9 = f32[5,32,128]{2,1,0:T(8,128)S(1)} collective-permute-done((f32[5,32,128]{2,1,0:T(8,128)S(1)}, f32[5,32,128]{2,1,0:T(8,128)S(1)}, u32[]{:S(2)}, u32[]{:S(2)}) %collective-permute-start.9) | collective-permute-done | bytes 81952 | tf_op jit(solution)/shard_map/ppermute | solution.py:27
  105.9 0.3 fusion.3
  106.6 0.9 copy.425
  (219 shorter events, 12.2 us)
Async XLA Ops:
  0.6 12.4 %copy-start.5 = (s32[128]{0:T(128)S(1)}, s32[128]{0:T(128)}, u32[]{:S(2)}) copy-start(s32[128]{0:T(128)} %param.11) | copy-start | bytes 1540
  0.6 12.4 %copy-start.4 = (f32[1,2,5,5]{3,1,2,0:T(2,128)S(1)}, f32[1,2,5,5]{3,1,2,0:T(2,128)}, u32[]{:S(2)}) copy-start(f32[1,2,5,5]{3,1,2,0:T(2,128)} %param.10) | copy-start | bytes 604
  1.8 17.1 %collective-permute-start = (f32[5,1,32,128]{3,2,0,1:T(8,128)S(1)}, f32[5,1,32,128]{3,2,0,1:T(8,128)S(1)}, u32[]{:S(2)}, u32[]{:S(2)}) collective-permute-start(f32[5,1,32,128]{3,2,0,1:T(8,128)S(1)} %get-tuple-element.18), channel_id=1, source_target_pairs={{1,0},{2,1},{3,2},{16,3},{17,16},{18,17},{19,18},{5,4},{6,5},{7,6}... | collective-permute-start | bytes 245768 | tf_op jit(solution)/shard_map/ppermute | solution.py:19
  3.1 15.8 %collective-permute-start.1 = (f32[5,1,32,128]{3,2,0,1:T(8,128)S(1)}, f32[5,1,32,128]{3,2,0,1:T(8,128)S(1)}, u32[]{:S(2)}, u32[]{:S(2)}) collective-permute-start(f32[5,1,32,128]{3,2,0,1:T(8,128)S(1)} %get-tuple-element.19), channel_id=1, source_target_pairs={{0,1},{1,2},{2,3},{3,16},{16,17},{17,18},{18,19},{4,5},{5,6},{6,7}... | collective-permute-start | bytes 245768 | tf_op jit(solution)/shard_map/ppermute | solution.py:16
  8.7 5.7 %collective-permute-start.2 = (f32[5,8,1,128]{3,2,0,1:T(1,128)S(1)}, f32[5,8,1,128]{3,2,0,1:T(1,128)S(1)}, u32[]{:S(2)}, u32[]{:S(2)}) collective-permute-start(f32[5,8,1,128]{3,2,0,1:T(1,128)S(1)} %get-tuple-element.14), channel_id=1, source_target_pairs={{4,0},{8,4},{12,8},{0,12},{5,1},{9,5},{13,9},{1,13},{6,2},{10,6},{... | collective-permute-start | bytes 61448 | tf_op jit(solution)/shard_map/ppermute | solution.py:19
  12.8 5.6 %collective-permute-start.3 = (f32[5,8,1,128]{3,2,0,1:T(1,128)S(1)}, f32[5,8,1,128]{3,2,0,1:T(1,128)S(1)}, u32[]{:S(2)}, u32[]{:S(2)}) collective-permute-start(f32[5,8,1,128]{3,2,0,1:T(1,128)S(1)} %get-tuple-element.15), channel_id=1, source_target_pairs={{0,4},{4,8},{8,12},{12,0},{1,5},{5,9},{9,13},{13,1},{2,6},{6,10},{... | collective-permute-start | bytes 61448 | tf_op jit(solution)/shard_map/ppermute | solution.py:16
  12.8 20.8 %copy-start.1 = (f32[1,5,5]{2,0,1:T(1,128)S(1)}, f32[1,5,5]{2,0,1:T(1,128)}, u32[]{:S(2)}) copy-start(f32[1,5,5]{2,0,1:T(1,128)} %param.9) | copy-start | bytes 304
  33.5 2.9 %copy-start.3 = (f32[1,5,8,32,128]{4,3,2,1,0:T(8,128)S(1)}, f32[1,5,8,32,128]{4,3,2,1,0:T(8,128)}, u32[]{:S(2)}) copy-start(f32[1,5,8,32,128]{4,3,2,1,0:T(8,128)} %param.7) | copy-start | bytes 1966084
  35.1 3.5 %copy-start = (f32[1,5,5,8,32,128]{5,4,3,2,1,0:T(8,128)S(1)}, f32[1,5,5,8,32,128]{5,4,3,2,1,0:T(8,128)}, u32[]{:S(2)}) copy-start(f32[1,5,5,8,32,128]{5,4,3,2,1,0:T(8,128)} %param.8) | copy-start | bytes 9830404
  41.2 6.6 %collective-permute-start.4 = (f32[5,32,128]{2,0,1:T(8,128)S(1)}, f32[5,32,128]{2,0,1:T(8,128)S(1)}, u32[]{:S(2)}, u32[]{:S(2)}) collective-permute-start(f32[5,32,128]{2,0,1:T(8,128)S(1)} %copy.310), channel_id=1, source_target_pairs={{0,1},{1,2},{2,3},{4,5},{5,6},{6,7},{8,9},{9,10},{10,11},{12,13},{... | collective-permute-start | bytes 245768 | tf_op jit(solution)/shard_map/ppermute | solution.py:27
  50.8 6.9 %collective-permute-start.5 = (f32[5,32,128]{2,0,1:T(8,128)S(1)}, f32[5,32,128]{2,0,1:T(8,128)S(1)}, u32[]{:S(2)}, u32[]{:S(2)}) collective-permute-start(f32[5,32,128]{2,0,1:T(8,128)S(1)} %copy.326), channel_id=1, source_target_pairs={{0,1},{1,2},{2,3},{4,5},{5,6},{6,7},{8,9},{9,10},{10,11},{12,13},{... | collective-permute-start | bytes 245768 | tf_op jit(solution)/shard_map/ppermute | solution.py:27
  60.6 6.9 %collective-permute-start.6 = (f32[5,32,128]{2,0,1:T(8,128)S(1)}, f32[5,32,128]{2,0,1:T(8,128)S(1)}, u32[]{:S(2)}, u32[]{:S(2)}) collective-permute-start(f32[5,32,128]{2,0,1:T(8,128)S(1)} %copy.342), channel_id=1, source_target_pairs={{0,1},{1,2},{2,3},{4,5},{5,6},{6,7},{8,9},{9,10},{10,11},{12,13},{... | collective-permute-start | bytes 245768 | tf_op jit(solution)/shard_map/ppermute | solution.py:27
  73.2 7.3 %collective-permute-start.7 = (f32[5,32,128]{2,0,1:T(8,128)S(1)}, f32[5,32,128]{2,0,1:T(8,128)S(1)}, u32[]{:S(2)}, u32[]{:S(2)}) collective-permute-start(f32[5,32,128]{2,0,1:T(8,128)S(1)} %copy_subtract_fusion), channel_id=1, source_target_pairs={{1,0},{2,1},{3,2},{5,4},{6,5},{7,6},{9,8},{10,9},{11,10},{13,12},{... | collective-permute-start | bytes 245768 | tf_op jit(solution)/shard_map/ppermute | solution.py:27
  83.7 9.5 %collective-permute-start.8 = (f32[5,32,128]{2,0,1:T(8,128)S(1)}, f32[5,32,128]{2,0,1:T(8,128)S(1)}, u32[]{:S(2)}, u32[]{:S(2)}) collective-permute-start(f32[5,32,128]{2,0,1:T(8,128)S(1)} %copy_subtract_fusion.1), channel_id=1, source_target_pairs={{1,0},{2,1},{3,2},{5,4},{6,5},{7,6},{9,8},{10,9},{11,10},{13,12},{... | collective-permute-start | bytes 245768 | tf_op jit(solution)/shard_map/ppermute | solution.py:27
  96.2 7.0 %collective-permute-start.9 = (f32[5,32,128]{2,1,0:T(8,128)S(1)}, f32[5,32,128]{2,1,0:T(8,128)S(1)}, u32[]{:S(2)}, u32[]{:S(2)}) collective-permute-start(f32[5,32,128]{2,1,0:T(8,128)S(1)} %sub.223), channel_id=1, source_target_pairs={{1,0},{2,1},{3,2},{5,4},{6,5},{7,6},{9,8},{10,9},{11,10},{13,12},{... | collective-permute-start | bytes 245768 | tf_op jit(solution)/shard_map/ppermute | solution.py:27
  104.7 1.7 %copy-start.2 = (f32[1,5,8,32,128]{4,3,2,1,0:T(8,128)S(1)}, f32[1,5,8,32,128]{4,3,2,1,0:T(8,128)}, u32[]{:S(2)}) copy-start(f32[1,5,8,32,128]{4,3,2,1,0:T(8,128)} %param.6) | copy-start | bytes 1966084
where the time goes:
time: 108 us; the launch traced here: 107 us
  waiting for transfers between devices  31.2 us (29%)
  starting transfers between devices  28 us (26%)
  matrix products  22.6 us (21%)
  blocking collectives  14.3 us (13%)
  local copies, waits for them, and re-layouts  4.66 us (4%)
  other arithmetic  4.12 us (4%)
  between operations  2.52 us (2%)
    ppermute x6, waiting for transfers between devices, shifted(): return lax.ppermute(block, axis, route)  25.9 us
    dot_general x66, matrix products, mix_const(): return jnp.einsum('ij,j...->i...', matrix, field, precision=exact_mode)  22.3 us
    ppermute x6, starting transfers between devices, shifted(): return lax.ppermute(block, axis, route)  17.1 us
    all_gather x1, blocking collectives, per_device(): candidates = lax.all_gather(partner, 'sector', axis=1, tiled=True)  14.3 us
    ppermute x2, starting transfers between devices, extended(): lax.ppermute(lax.slice_in_dim(block, block.shape[dim] - width, None, axis...  5.51 us
    ppermute x2, starting transfers between devices, extended(): lax.ppermute(lax.slice_in_dim(block, 0, width, axis=dim), axis, backward)  5.47 us
    ppermute x2, waiting for transfers between devices, extended(): lax.ppermute(lax.slice_in_dim(block, block.shape[dim] - width, None, axis...  4.1 us
    unnamed x21, local copies, waits for them, and re-layouts  3.07 us
  transfers between devices with their start and end apart: 10, of which 8 were waited for; matrix products, arithmetic and copies ran while one was open for 2% of the time, Pallas kernels for 0%

commit v1 on v0

v1 whole, which is shorter than its diff:
```python
import functools

import jax
import jax.numpy as jnp
from jax import lax
from jax.experimental import pallas as pl
from jax.experimental.pallas import tpu as pltpu
from jax.sharding import PartitionSpec as P

MESH = pl.DeviceIdType.MESH
PAD = 8
GROUP = 8


def total(terms):
    while len(terms) > 1:
        pairs = [a + b for a, b in zip(terms[::2], terms[1::2])]
        if len(terms) % 2:
            pairs.append(terms[-1])
        terms = pairs
    return terms[0]


def kernel(
    sectors, slabs,
    state, source, inverse, axial, cross, picks,
    residual_out, state_out,
    q, src, inv, eff, res, prov, upd, facing, entering, following,
    local_sem, out_sem, ax_send, ax_recv, se_send, se_recv,
    if_send, if_recv, fw_send, fw_recv, bw_send, bw_recv,
):
    nv, planes, columns, cells = src.shape
    groups = columns // GROUP
    row = lax.axis_index("row")
    sector = lax.axis_index("sector")
    slab = lax.axis_index("slab")
    has_low = slab > 0
    has_high = slab < slabs - 1
    rotor_top = jnp.logical_and(row == 0, slab == slabs - 1)
    stator_foot = jnp.logical_and(row == 1, slab == 0)
    on_plane = jnp.logical_or(rotor_top, stator_foot)
    after = lax.rem(sector + 1, sectors)
    before = lax.rem(sector + sectors - 1, sectors)
    facing_slab = jnp.where(row == 0, 0, slabs - 1)
    body = pl.ds(PAD, columns)

    load_state = pltpu.make_async_copy(
        state.at[0], q.at[:, pl.ds(1, planes), body], local_sem.at[0]
    )
    load_state.start()
    load_inverse = pltpu.make_async_copy(inverse.at[0], inv, local_sem.at[2])
    load_inverse.start()
    load_source = pltpu.make_async_copy(source.at[0], src, local_sem.at[1])
    load_source.start()

    barrier = pltpu.get_barrier_semaphore()

    def greet(**where):
        pl.semaphore_signal(barrier, inc=1, device_id=where, device_id_type=MESH)

    @pl.when(on_plane)
    def _():
        for other in range(sectors):
            greet(row=1 - row, sector=other, slab=facing_slab)

    greet(sector=after)
    greet(sector=before)

    @pl.when(has_low)
    def _():
        greet(slab=slab - 1)

    @pl.when(has_high)
    def _():
        greet(slab=slab + 1)

    zero_plane = jnp.zeros((nv, columns, cells), jnp.float32)

    @pl.when(jnp.logical_not(has_low))
    def _():
        q[:, 0, body] = zero_plane

    @pl.when(jnp.logical_not(has_high))
    def _():
        q[:, planes + 1, body] = zero_plane

    peers = 2 + has_low.astype(jnp.int32) + has_high.astype(jnp.int32)
    pl.semaphore_wait(barrier, peers + jnp.where(on_plane, sectors, 0))

    load_state.wait()

    def remote(source_ref, target_ref, send, recv, **where):
        return pltpu.make_async_remote_copy(
            src_ref=source_ref, dst_ref=target_ref, send_sem=send, recv_sem=recv,
            device_id=where, device_id_type=MESH,
        )

    def facing_copy(plane_at, other):
        return remote(
            q.at[:, plane_at, body], facing.at[sector], if_send.at[other], if_recv.at[sector],
            row=1 - row, sector=other, slab=facing_slab,
        )

    def facing_arrival(other):
        return remote(
            q.at[:, 1, body], facing.at[other], if_send.at[other], if_recv.at[other],
            row=1 - row, sector=other, slab=facing_slab,
        )

    @pl.when(rotor_top)
    def _():
        for other in range(sectors):
            facing_copy(planes, other).start()

    @pl.when(stator_foot)
    def _():
        for other in range(sectors):
            facing_copy(1, other).start()

    inner = pl.ds(1, planes)
    to_after = remote(
        q.at[:, inner, pl.ds(PAD + columns - 1, 1)], q.at[:, inner, pl.ds(PAD - 1, 1)],
        se_send.at[0], se_recv.at[0], sector=after,
    )
    to_before = remote(
        q.at[:, inner, pl.ds(PAD, 1)], q.at[:, inner, pl.ds(PAD + columns, 1)],
        se_send.at[1], se_recv.at[1], sector=before,
    )
    to_after.start()
    to_before.start()
    to_high = remote(
        q.at[:, planes, body], q.at[:, 0, body], ax_send.at[0], ax_recv.at[0], slab=slab + 1
    )
    to_low = remote(
        q.at[:, 1, body], q.at[:, planes + 1, body], ax_send.at[1], ax_recv.at[1], slab=slab - 1
    )

    @pl.when(has_high)
    def _():
        to_high.start()

    @pl.when(has_low)
    def _():
        to_low.start()

    load_inverse.wait()

    def effective(x, carry):
        for i in range(nv):
            blocks = [inv[i, j, x] for j in range(nv)]
            for k in range(nv):
                eff[i, k, x] = total([blocks[j] * (0.5 * axial[0, j, k]) for j in range(nv)])
        return carry

    lax.fori_loop(0, planes, effective, 0)
    load_source.wait()
    to_after.wait_recv()
    to_before.wait_recv()

    @pl.when(has_high)
    def _():
        to_low.wait_recv()

    @pl.when(has_low)
    def _():
        to_high.wait_recv()

    def gather_facing(target):
        for other in range(sectors):
            facing_arrival(other).wait_recv()

        def pick(c, carry):
            at = picks[c]
            part, column = at // columns, lax.rem(at, columns)
            for v in range(nv):
                target[v, pl.ds(c, 1)] = facing[part, v, pl.ds(column, 1)]
            return carry

        lax.fori_loop(0, columns, pick, 0)

    @pl.when(rotor_top)
    def _():
        gather_facing(q.at[:, planes + 1, body])

    lane = lax.broadcasted_iota(jnp.int32, (columns, cells), 1)

    def flux(x, carry):
        sums = [None] * nv
        for v in range(nv):
            here = q[v, x + 1, body]
            spans = (
                q[v, x + 2, body] - q[v, x, body],
                q[v, x + 1, pl.ds(PAD + 1, columns)] - q[v, x + 1, pl.ds(PAD - 1, columns)],
                jnp.where(lane == cells - 1, 0.0, pltpu.roll(here, cells - 1, 1))
                - jnp.where(lane == 0, 0.0, pltpu.roll(here, 1, 1)),
            )
            for i in range(nv):
                factors = (axial[0, i, v], cross[0, 0, i, v], cross[0, 1, i, v])
                term = total([(0.5 * f) * s for f, s in zip(factors, spans)])
                sums[i] = term if sums[i] is None else sums[i] + term
        values = [src[i, x] - sums[i] for i in range(nv)]
        for i in range(nv):
            res[i, x] = values[i]
        for i in range(nv):
            prov[i, x] = total([inv[i, j, x] * values[j] for j in range(nv)])
        return carry

    lax.fori_loop(0, planes, flux, 0)

    def residual_copy():
        return pltpu.make_async_copy(res, residual_out.at[0], out_sem.at[0])

    @pl.when(jnp.logical_not(stator_foot))
    def _():
        residual_copy().start()

    @pl.when(jnp.logical_not(has_low))
    def _():
        entering[...] = zero_plane

    @pl.when(jnp.logical_not(has_high))
    def _():
        following[...] = zero_plane

    @pl.when(stator_foot)
    def _():
        gather_facing(entering)

    def columns_of(k):
        return pl.ds(pl.multiple_of(k * GROUP, GROUP), GROUP)

    def forward_copy(k):
        return remote(
            prov.at[:, planes - 1, columns_of(k)], entering.at[:, columns_of(k)],
            fw_send.at[k], fw_recv.at[k], slab=slab + 1,
        )

    def backward_copy(k):
        return remote(
            upd.at[:, 0, columns_of(k)], following.at[:, columns_of(k)],
            bw_send.at[k], bw_recv.at[k], slab=slab - 1,
        )

    def forward(k, carry):
        @pl.when(has_low)
        def _():
            forward_copy(k).wait_recv()

        at = columns_of(k)
        now = [entering[v, at] for v in range(nv)]
        for x in range(planes):
            now = [
                total([prov[i, x, at]] + [eff[i, j, x, at] * now[j] for j in range(nv)])
                for i in range(nv)
            ]
            for i in range(nv):
                prov[i, x, at] = now[i]

        @pl.when(has_high)
        def _():
            forward_copy(k).start()

        return carry

    lax.fori_loop(0, groups, forward, 0)

    @pl.when(stator_foot)
    def _():
        ghost = [entering[v] for v in range(nv)]
        for i in range(nv):
            res[i, 0] = res[i, 0] + total(
                [(0.5 * axial[0, i, j]) * ghost[j] for j in range(nv)]
            )
        residual_copy().start()

    def state_copy(k):
        at = columns_of(k)
        return pltpu.make_async_copy(
            q.at[:, pl.ds(1, planes), pl.ds(pl.multiple_of(PAD + k * GROUP, GROUP), GROUP)],
            state_out.at[0, :, :, at], out_sem.at[1 + k],
        )

    def backward(k, carry):
        @pl.when(has_high)
        def _():
            backward_copy(k).wait_recv()

        at = columns_of(k)
        shifted = pl.ds(pl.multiple_of(PAD + k * GROUP, GROUP), GROUP)
        now = [following[v, at] for v in range(nv)]
        for x in reversed(range(planes)):
            now = [
                prov[i, x, at] - total([eff[i, j, x, at] * now[j] for j in range(nv)])
                for i in range(nv)
            ]
            if x == 0:
                for i in range(nv):
                    upd[i, 0, at] = now[i]

                @pl.when(has_low)
                def _():
                    backward_copy(k).start()

            for i in range(nv):
                q[i, x + 1, shifted] = q[i, x + 1, shifted] + now[i]
        state_copy(k).start()
        return carry

    to_after.wait_send()
    to_before.wait_send()

    @pl.when(has_high)
    def _():
        to_high.wait_send()

    @pl.when(has_low)
    def _():
        to_low.wait_send()

    @pl.when(on_plane)
    def _():
        for other in range(sectors):
            facing_copy(1, other).wait_send()

    lax.fori_loop(0, groups, backward, 0)

    def finish(k, carry):
        @pl.when(has_high)
        def _():
            forward_copy(k).wait_send()

        @pl.when(has_low)
        def _():
            backward_copy(k).wait_send()

        state_copy(k).wait()
        return carry

    lax.fori_loop(0, groups, finish, 0)
    residual_copy().wait()


def per_device(state, source, diag_inverse, jac_axial, jac_cross, owner):
    _, nv, planes, columns, cells = state.shape
    sectors = lax.axis_size("sector")
    slabs = lax.axis_size("slab")
    groups = columns // GROUP
    row = lax.axis_index("row")
    first = lax.axis_index("sector") * columns
    ids = first + jnp.arange(columns, dtype=jnp.int32)
    everyone = jnp.arange(owner.shape[0], dtype=jnp.int32)
    hits = jnp.where(
        row == 0, everyone[None, :] == ids[:, None], owner[None, :] == ids[:, None]
    )
    values = jnp.where(row == 0, owner, everyone)
    picks = jnp.sum(jnp.where(hits, values[None, :], 0), axis=1)

    def vmem(*shape):
        return pltpu.VMEM(shape, jnp.float32)

    dma = pltpu.SemaphoreType.DMA
    field = (nv, planes, columns, cells)
    plane = (nv, columns, cells)
    anywhere = pl.BlockSpec(memory_space=pl.ANY)
    scalars = pl.BlockSpec(memory_space=pltpu.SMEM)
    return pl.pallas_call(
        functools.partial(kernel, sectors, slabs),
        out_shape=[jax.ShapeDtypeStruct(state.shape, jnp.float32)] * 2,
        in_specs=[anywhere] * 3 + [scalars] * 3,
        out_specs=[anywhere] * 2,
        scratch_shapes=[
            vmem(nv, planes + 2, columns + 2 * PAD, cells),
            vmem(*field),
            vmem(nv, *field),
            vmem(nv, *field),
            vmem(*field),
            vmem(*field),
            vmem(nv, 1, columns, cells),
            vmem(sectors, *plane),
            vmem(*plane),
            vmem(*plane),
            dma((3,)), dma((1 + groups,)),
            dma((2,)), dma((2,)), dma((2,)), dma((2,)),
            dma((sectors,)), dma((sectors,)),
            dma((groups,)), dma((groups,)), dma((groups,)), dma((groups,)),
        ],
        compiler_params=pltpu.CompilerParams(collective_id=0, has_side_effects=True),
    )(state, source, diag_inverse, jac_axial, jac_cross, picks)


def solution(mesh):
    return jax.shard_map(
        per_device,
        mesh=mesh,
        in_specs=(
            P("row", None, "slab", "sector", None),
            P("row", None, "slab", "sector", None),
            P("row", None, None, "slab", "sector", None),
            P("row", None, None),
            P("row", None, None, None),
            P(),
        ),
        out_specs=(P("row", None, "slab", "sector", None), P("row", None, "slab", "sector", None)),
        check_vma=False,
    )
```

time: 108 us -> 43.7 us (0.40)
  Pallas kernels: 0 us -> 34.1 us
  waiting for transfers between devices: 31.2 us -> 0 us
  starting transfers between devices: 28 us -> 0 us
  matrix products: 22.6 us -> 0 us
  blocking collectives: 14.3 us -> 0 us
  other arithmetic: 4.12 us -> 2.05 us
  local copies, waits for them, and re-layouts: 4.66 us -> 6.54 us
  between operations: 2.52 us -> 0.65 us
    pallas_call x0 -> x1, Pallas kernels: none -> 34.1 us  [per_device(): pl.pallas_call(functools.partial(kernel, sectors, slabs), out_shape=[jax....]
    ppermute x10 -> x0, waiting for transfers between devices: 31.2 us -> none  [the longest x6 25.9 us: shifted(): return lax.ppermute(block, axis, route)]
    ppermute x10 -> x0, starting transfers between devices: 28 us -> none  [the longest x6 17.1 us: shifted(): return lax.ppermute(block, axis, route)]
    dot_general x67 -> x0, matrix products: 22.6 us -> none  [the longest x66 22.3 us: mix_const(): return jnp.einsum('ij,j...->i...', matrix, field, precision=exact_mode)]
    all_gather x1 -> x0, blocking collectives: 14.3 us -> none  [per_device(): candidates = lax.all_gather(partner, 'sector', axis=1, tiled=True)]
    unnamed x21 -> x4, local copies, waits for them, and re-layouts: 3.07 us -> 6.54 us
    reduce_sum x63 -> x1, other arithmetic: 2.7 us -> 1.38 us  [per_device(): picks = jnp.sum(jnp.where(hits, values[None, :], 0), axis=1)]
    sub x33 -> x0, other arithmetic: 1.27 us -> none  [the longest x31 0.66 us: backward_sweep(): provisional[:, plane_at]]
  transfers between devices with their start and end apart: 10 -> 0, of which waited for: 8 -> 0; matrix products, arithmetic and copies ran while one was open for 2% -> 0% of each run, Pallas kernels for 0% -> 0%
where the time goes in v1:
time: 43.7 us; the launch traced here: 43.4 us
  Pallas kernels  34.1 us (78%)
  local copies, waits for them, and re-layouts  6.54 us (15%)
  other arithmetic  2.05 us (5%)
  between operations  0.65 us (1%)
    pallas_call x1, Pallas kernels, per_device(): pl.pallas_call(functools.partial(kernel, sectors, slabs), out_shape=[jax....  34.1 us
    unnamed x4, local copies, waits for them, and re-layouts  6.54 us
    reduce_sum x1, other arithmetic, per_device(): picks = jnp.sum(jnp.where(hits, values[None, :], 0), axis=1)  1.38 us

profile of v1, /device:TPU:0, one launch (start us, length us, event | category | flops | bytes accessed | tf_op | source)
XLA Modules:
  0.0 43.4 jit_solution(13566784607184886831)
XLA Ops:
  0.6 0.7 %broadcast_select_fusion = s32[128]{0:T(128)S(1)} fusion(s32[128]{0:T(128)} %param.11, pred[]{:T(512)S(6)} %eq.12), kind=kLoop, calls=%fused_computation.3 | loop fusion | flops 128 | bytes 1025 | tf_op jit(solution)/shard_map/jit(_where)/select_n | solution.py:355
  1.3 1.4 %select_reduce_fusion.picks = s32[32]{0:T(128)} fusion(s32[128]{0:T(128)S(1)} %broadcast_select_fusion, s32[128]{0:T(128)} %param.11, s32[32]{0:T(128)S(1)} %iota_add_fusion, pred[]{:T(512)S(6)} %eq.12), kind=kLoop, calls=%fused_computation | loop fusion | flops 20448 | bytes 1281 | tf_op jit(solution)/shard_map/reduce_sum | solution.py:356
  2.7 1.3 %copy.10.axial = f32[1,5,5]{2,1,0:T(8,128)} copy(f32[1,5,5]{2,0,1:T(1,128)} %param.9) | data formatting | bytes 200 | tf_op args[3]
  4.0 1.3 %copy.11.cross = f32[1,2,5,5]{3,2,1,0:T(8,128)} copy(f32[1,2,5,5]{3,1,2,0:T(2,128)} %param.10) | data formatting | bytes 400 | tf_op args[4]
  5.3 34.1 %shard_map.77 = (f32[1,5,8,32,128]{4,3,2,1,0:T(8,128)}, f32[1,5,8,32,128]{4,3,2,1,0:T(8,128)}) custom-call(f32[1,5,8,32,128]{4,3,2,1,0:T(8,128)} %state.1, f32[1,5,8,32,128]{4,3,2,1,0:T(8,128)} %source.1, f32[1,5,5,8,32,128]{5,4,3,2,1,0:T(8,128)} %inverse.1, f32[1,5,5]{2,1,0:T(8,128)} %copy.10.axial, f32[1,2,5,5]{3,2,1,0:T(8,128)} %copy.11.cross, ...), custom_call_target="tpu_custom_call" | custom-call | tf_op jit(solution)/shard_map/pallas_call | solution.py:366
  39.4 2.0 %copy.14 = f32[1,5,8,32,128]{4,3,2,1,0:T(8,128)} copy(f32[1,5,8,32,128]{4,3,2,1,0:T(8,128)} %get-tuple-element.4) | data formatting | bytes 1310720
  41.4 2.0 %copy.15 = f32[1,5,8,32,128]{4,3,2,1,0:T(8,128)} copy(f32[1,5,8,32,128]{4,3,2,1,0:T(8,128)} %get-tuple-element.5) | data formatting | bytes 1310720
  (1 shorter events, 0.0 us)

commit v2 on v1

--- a/solution.py
+++ b/solution.py
@@ -23,10 +23,11 @@
 
 def kernel(
     sectors, slabs,
-    state, source, inverse, axial, cross, picks,
-    residual_out, state_out,
-    q, src, inv, eff, res, prov, upd, facing, entering, following,
-    local_sem, out_sem, ax_send, ax_recv, se_send, se_recv,
+    state, source, inverse, axial_in, cross_in, owner_in,
+    res_out, state_out,
+    axial, cross, owner, picks_wide, picks,
+    q, src, inv, eff, prov, upd, facing, entering, following,
+    local_sem, ax_send, ax_recv, se_send, se_recv,
     if_send, if_recv, fw_send, fw_recv, bw_send, bw_recv,
 ):
     nv, planes, columns, cells = src.shape
@@ -48,6 +49,12 @@
         state.at[0], q.at[:, pl.ds(1, planes), body], local_sem.at[0]
     )
     load_state.start()
+    load_owner = pltpu.make_async_copy(owner_in, owner, local_sem.at[3])
+    load_owner.start()
+    load_axial = pltpu.make_async_copy(axial_in, axial, local_sem.at[4])
+    load_axial.start()
+    load_cross = pltpu.make_async_copy(cross_in, cross, local_sem.at[5])
+    load_cross.start()
     load_inverse = pltpu.make_async_copy(inverse.at[0], inv, local_sem.at[2])
     load_inverse.start()
     load_source = pltpu.make_async_copy(source.at[0], src, local_sem.at[1])
@@ -84,6 +91,20 @@
     def _():
         q[:, planes + 1, body] = zero_plane
 
+    load_owner.wait()
+    shape = (columns, owner.shape[1])
+    ids = sector * columns + lax.broadcasted_iota(jnp.int32, shape, 0)
+    everyone = lax.broadcasted_iota(jnp.int32, shape, 1)
+    owners = jnp.broadcast_to(owner[...], shape)
+    is_rotor = jnp.broadcast_to(row, shape) == 0
+    hits = jnp.where(is_rotor, everyone, owners) == ids
+    found = jnp.sum(
+        jnp.where(hits, jnp.where(is_rotor, owners, everyone), 0), axis=1, keepdims=True
+    )
+    found = jnp.minimum(found, owner.shape[1] - 1)
+    picks_wide[...] = jnp.broadcast_to(found, picks_wide.shape)
+    move_picks = pltpu.make_async_copy(picks_wide, picks, local_sem.at[6])
+    move_picks.start()
     peers = 2 + has_low.astype(jnp.int32) + has_high.astype(jnp.int32)
     pl.semaphore_wait(barrier, peers + jnp.where(on_plane, sectors, 0))
 
@@ -144,12 +165,15 @@
         to_low.start()
 
     load_inverse.wait()
+    load_axial.wait()
+    load_cross.wait()
+    move_picks.wait()
 
     def effective(x, carry):
         for i in range(nv):
             blocks = [inv[i, j, x] for j in range(nv)]
             for k in range(nv):
-                eff[i, k, x] = total([blocks[j] * (0.5 * axial[0, j, k]) for j in range(nv)])
+                eff[i, k, x] = total([blocks[j] * (0.5 * axial[j, 0, k]) for j in range(nv)])
         return carry
 
     lax.fori_loop(0, planes, effective, 0)
@@ -170,7 +194,7 @@
             facing_arrival(other).wait_recv()
 
         def pick(c, carry):
-            at = picks[c]
+            at = picks[c, 0]
             part, column = at // columns, lax.rem(at, columns)
             for v in range(nv):
                 target[v, pl.ds(c, 1)] = facing[part, v, pl.ds(column, 1)]
@@ -195,24 +219,17 @@
                 - jnp.where(lane == 0, 0.0, pltpu.roll(here, 1, 1)),
             )
             for i in range(nv):
-                factors = (axial[0, i, v], cross[0, 0, i, v], cross[0, 1, i, v])
+                factors = (axial[i, 0, v], cross[0, i, 0, v], cross[0, i, 1, v])
                 term = total([(0.5 * f) * s for f, s in zip(factors, spans)])
                 sums[i] = term if sums[i] is None else sums[i] + term
         values = [src[i, x] - sums[i] for i in range(nv)]
         for i in range(nv):
-            res[i, x] = values[i]
+            res_out[0, i, x] = values[i]
         for i in range(nv):
             prov[i, x] = total([inv[i, j, x] * values[j] for j in range(nv)])
         return carry
 
     lax.fori_loop(0, planes, flux, 0)
-
-    def residual_copy():
-        return pltpu.make_async_copy(res, residual_out.at[0], out_sem.at[0])
-
-    @pl.when(jnp.logical_not(stator_foot))
-    def _():
-        residual_copy().start()
 
     @pl.when(jnp.logical_not(has_low))
     def _():
@@ -268,17 +285,9 @@
     def _():
         ghost = [entering[v] for v in range(nv)]
         for i in range(nv):
-            res[i, 0] = res[i, 0] + total(
-                [(0.5 * axial[0, i, j]) * ghost[j] for j in range(nv)]
+            res_out[0, i, 0] = res_out[0, i, 0] + total(
+                [(0.5 * axial[i, 0, j]) * ghost[j] for j in range(nv)]
             )
-        residual_copy().start()
-
-    def state_copy(k):
-        at = columns_of(k)
-        return pltpu.make_async_copy(
-            q.at[:, pl.ds(1, planes), pl.ds(pl.multiple_of(PAD + k * GROUP, GROUP), GROUP)],
-            state_out.at[0, :, :, at], out_sem.at[1 + k],
-        )
 
     def backward(k, carry):
         @pl.when(has_high)
@@ -302,8 +311,7 @@
                     backward_copy(k).start()
 
             for i in range(nv):
-                q[i, x + 1, shifted] = q[i, x + 1, shifted] + now[i]
-        state_copy(k).start()
+                state_out[0, i, x, at] = q[i, x + 1, shifted] + now[i]
         return carry
 
     to_after.wait_send()
@@ -333,11 +341,9 @@
         def _():
             backward_copy(k).wait_send()
 
-        state_copy(k).wait()
         return carry
 
     lax.fori_loop(0, groups, finish, 0)
-    residual_copy().wait()
 
 
 def per_device(state, source, diag_inverse, jac_axial, jac_cross, owner):
@@ -345,16 +351,6 @@
     sectors = lax.axis_size("sector")
     slabs = lax.axis_size("slab")
     groups = columns // GROUP
-    row = lax.axis_index("row")
-    first = lax.axis_index("sector") * columns
-    ids = first + jnp.arange(columns, dtype=jnp.int32)
-    everyone = jnp.arange(owner.shape[0], dtype=jnp.int32)
-    hits = jnp.where(
-        row == 0, everyone[None, :] == ids[:, None], owner[None, :] == ids[:, None]
-    )
-    values = jnp.where(row == 0, owner, everyone)
-    picks = jnp.sum(jnp.where(hits, values[None, :], 0), axis=1)
-
     def vmem(*shape):
         return pltpu.VMEM(shape, jnp.float32)
 
@@ -362,30 +358,35 @@
     field = (nv, planes, columns, cells)
     plane = (nv, columns, cells)
     anywhere = pl.BlockSpec(memory_space=pl.ANY)
-    scalars = pl.BlockSpec(memory_space=pltpu.SMEM)
+    outside = pl.BlockSpec(memory_space=pltpu.HBM)
     return pl.pallas_call(
         functools.partial(kernel, sectors, slabs),
-        out_shape=[jax.ShapeDtypeStruct(state.shape, jnp.float32)] * 2,
-        in_specs=[anywhere] * 3 + [scalars] * 3,
-        out_specs=[anywhere] * 2,
+        out_shape=[vmem(*state.shape)] * 2,
+        in_specs=[outside] * 6,
+        out_specs=[pl.BlockSpec(memory_space=pltpu.VMEM)] * 2,
         scratch_shapes=[
+            pltpu.SMEM((nv, 1, nv), jnp.float32),
+            pltpu.SMEM((1, nv, 2, nv), jnp.float32),
+            pltpu.VMEM((1, owner.shape[0]), jnp.int32),
+            pltpu.VMEM((columns, 128), jnp.int32),
+            pltpu.SMEM((columns, 128), jnp.int32),
             vmem(nv, planes + 2, columns + 2 * PAD, cells),
             vmem(*field),
             vmem(nv, *field),
             vmem(nv, *field),
             vmem(*field),
-            vmem(*field),
             vmem(nv, 1, columns, cells),
             vmem(sectors, *plane),
             vmem(*plane),
             vmem(*plane),
-            dma((3,)), dma((1 + groups,)),
+            dma((7,)),
             dma((2,)), dma((2,)), dma((2,)), dma((2,)),
             dma((sectors,)), dma((sectors,)),
             dma((groups,)), dma((groups,)), dma((groups,)), dma((groups,)),
         ],
         compiler_params=pltpu.CompilerParams(collective_id=0, has_side_effects=True),
-    )(state, source, diag_inverse, jac_axial, jac_cross, picks)
+    )(state, source, diag_inverse, jnp.swapaxes(jac_axial, 0, 1),
+        jnp.swapaxes(jac_cross, 1, 2), owner[None])
 
 
 def solution(mesh):

time: 43.7 us -> 35.5 us (0.81)
  local copies, waits for them, and re-layouts: 6.54 us -> 1.67 us
  other arithmetic: 2.05 us -> 0 us
  Pallas kernels: 34.1 us -> 33.1 us
    unnamed x4 -> x2, local copies, waits for them, and re-layouts: 6.54 us -> 1.67 us
    reduce_sum x1 -> x0, other arithmetic: 1.38 us -> none  [per_device(): picks = jnp.sum(jnp.where(hits, values[None, :], 0), axis=1)]
    pallas_call x1, Pallas kernels: 34.1 us -> 33.1 us  [per_device(): pl.pallas_call(functools.partial(kernel, sectors, slabs), out_shape=[vmem...]
    select_n x1 -> x0, other arithmetic: 0.67 us -> none  [per_device(): values = jnp.where(row == 0, owner, everyone)]
where the time goes in v2:
time: 35.5 us; the launch traced here: 35.4 us
  Pallas kernels  33.1 us (93%)
  local copies, waits for them, and re-layouts  1.67 us (5%)
  between operations  0.64 us (2%)
    pallas_call x1, Pallas kernels, per_device(): pl.pallas_call(functools.partial(kernel, sectors, slabs), out_shape=[vmem...  33.1 us
    unnamed x2, local copies, waits for them, and re-layouts  1.67 us

profile of v2, /device:TPU:0, one launch (start us, length us, event | category | flops | bytes accessed | tf_op | source)
XLA Modules:
  0.0 35.4 jit_solution(15772680711455237516)
XLA Ops:
  0.6 33.1 %shard_map.77 = (f32[1,5,8,32,128]{4,3,2,1,0:T(8,128)S(1)}, f32[1,5,8,32,128]{4,3,2,1,0:T(8,128)S(1)}) custom-call(f32[1,5,8,32,128]{4,3,2,1,0:T(8,128)} %state.1, f32[1,5,8,32,128]{4,3,2,1,0:T(8,128)} %source.1, f32[1,5,5,8,32,128]{5,4,3,2,1,0:T(8,128)} %inverse.1, f32[5,1,5]{2,1,0:T(1,128)} %bitcast.4, f32[1,5,2,5]{3,2,1,0:T(2,128)} %bitcast.3, ...), custom_call_target="tpu_custom_call" | custom-call | tf_op jit(solution)/shard_map/pallas_call | solution.py:362
  33.7 0.8 %copy.10 = f32[1,5,8,32,128]{4,3,2,1,0:T(8,128)} copy(f32[1,5,8,32,128]{4,3,2,1,0:T(8,128)S(1)} %get-tuple-element.2) | data formatting | bytes 1310720
  34.5 0.8 %copy.11 = f32[1,5,8,32,128]{4,3,2,1,0:T(8,128)} copy(f32[1,5,8,32,128]{4,3,2,1,0:T(8,128)S(1)} %get-tuple-element.3) | data formatting | bytes 1310720
